TPU v7x, 32 devices: a whole 2x2x4 slice. The times are simulated.
32 devices in a mesh: grid: 8 (over z, y), atom: 4 (over x, core).
Axes of the slice: x: 2, y: 2, z: 4, core: 2. Of those that a mesh axis runs over, the one named last changes fastest.
Arguments:
- weights: float32 [524288], P(('grid', 'atom')), may hold values from 0.25 to 4
- target: float32 [524288], P(('grid', 'atom')), may hold values from -6 to 6
- coupling: float32 [524288], P(('grid', 'atom')), may hold values from -0.9 to 0.9
- multipole_basis: float32 [25, 524288], P(None, ('grid', 'atom')), may hold values from -6 to 6
- rho_hist: float32 [8, 524288], P(None, ('grid', 'atom')), may hold values from -6 to 6
- res_hist: float32 [8, 524288], P(None, ('grid', 'atom')), may hold values from -6 to 6
- batch_atom: int32 [2048], P(('grid', 'atom')), may hold values from 0 to 2047
- owner_slot: int32 [2048], replicated, may hold values from 0 to 2047, each once
- slot_index: int32 [2], replicated, may hold values from 0 to 7
Outputs:
- density: float32 [524288], P(('grid', 'atom'))
- moments: float32 [25, 2048], P(None, 'atom')
Inputs may be any that keep to these rules, and one draw needn't show every extreme that they name: `owner_slot`: each slot 0 to 2047 belongs to exactly one atom.
All inputs are finite; a program needn't handle non-finite values.
Results may differ from a plain program's by a relative error of at most 0.00011.
Values sent between devices are 32-bit elements; how exact they have to be, the bound alone decides.
A program may use at most 64 MiB of HBM per device.

v0:
```python
import functools
import math

import jax
import jax.numpy as jnp
from jax import lax
from jax.experimental import pallas as pl
from jax.experimental.pallas import tpu as pltpu
from jax.sharding import PartitionSpec as P

MESH = pl.DeviceIdType.MESH
LANES = 128
SUBS = 8
mixing_beta = 0.5
ridge_share = 0.1
F32 = jnp.float32


def solve_coeffs(entry, hist_len):
    trace = entry[0][0]
    for i in range(1, hist_len):
        trace = trace + entry[i][i]
    ridge = (ridge_share / hist_len) * trace
    low = [[entry[i][j] for j in range(i + 1)] for i in range(hist_len)]
    for i in range(hist_len):
        low[i][i] = low[i][i] + ridge
    inverse = [None] * hist_len
    factor = [[None] * hist_len for _ in range(hist_len)]
    forward = [jnp.ones_like(trace) for _ in range(hist_len)]
    for j in range(hist_len):
        inverse[j] = 1.0 / low[j][j]
        for i in range(j + 1, hist_len):
            factor[i][j] = low[i][j] * inverse[j]
        for i in range(j + 1, hist_len):
            forward[i] = forward[i] - factor[i][j] * forward[j]
            for k in range(j + 1, i + 1):
                low[i][k] = low[i][k] - factor[i][j] * low[k][j]
    backward = [forward[i] * inverse[i] for i in range(hist_len)]
    for j in reversed(range(hist_len)):
        for i in range(j):
            backward[i] = backward[i] - factor[j][i] * backward[j]
    total = backward[0]
    for i in range(1, hist_len):
        total = total + backward[i]
    return [backward[i] / total for i in range(hist_len)]


def split(x):
    pieces = []
    for _ in range(3):
        piece = x.astype(jnp.bfloat16).astype(F32)
        pieces.append(piece)
        x = x - piece
    return pieces


def kernel(
    cfg,
    batch_atom,
    owner_slot,
    slot_index,
    w_hbm,
    target_hbm,
    coupling_hbm,
    basis_hbm,
    rho_hbm,
    res_hbm,
    density_out,
    moments_out,
    w,
    target,
    coupling,
    basis,
    rho,
    res,
    fresh,
    fresh_w,
    row_bufs,
    moment_bufs,
    near,
    own,
    hist_moments,
    base_rows,
    correct,
    load_sem,
    send_sem,
    recv_sem,
):
    iters, hist_len, harmonics, batches, width, owned, groups, members, scale = cfg
    devices = groups * members
    tiles = w.shape[0]
    per_batch = width // LANES
    half = LANES // 2
    rows = batches // 4
    my_group = lax.axis_index("grid")
    my_member = lax.axis_index("atom")
    me = my_group * members + my_member

    def peer(step):
        spot = lax.rem(me + step, devices)
        return spot, (lax.div(spot, members), lax.rem(spot, members))

    barrier = pltpu.get_barrier_semaphore()

    @pl.loop(1, devices)
    def _(step):
        pl.semaphore_signal(barrier, inc=1, device_id=peer(step)[1], device_id_type=MESH)

    loads = [
        pltpu.make_async_copy(src, dst, load_sem.at[k])
        for k, (src, dst) in enumerate(
            ((res_hbm, res), (w_hbm, w), (basis_hbm, basis), (rho_hbm, rho), (target_hbm, target), (coupling_hbm, coupling))
        )
    ]
    for load in loads:
        load.start()

    lane = lax.broadcasted_iota(jnp.int32, (SUBS, LANES), 1)
    sub = lax.broadcasted_iota(jnp.int32, (SUBS, LANES), 0)
    quarter = lane // 32
    lane_row = lax.broadcasted_iota(jnp.int32, (1, LANES), 1)

    slot_row = jnp.zeros((1, LANES), F32)
    slot_cols = []
    for block in range(batches // SUBS):
        col = jnp.zeros((SUBS, LANES), F32)
        for at in range(SUBS):
            b = block * SUBS + at
            slot = owner_slot[batch_atom[b]].astype(F32)
            slot_row = jnp.where(lane_row == half + b, slot, slot_row)
            col = jnp.where(sub == at, slot, col)
        slot_cols.append(col)
    slot_col = jnp.concatenate(slot_cols, axis=0)

    def lane_tile(t):
        return pl.ds(pl.multiple_of(t * LANES, LANES), LANES)

    def exchange(buf, which):
        def copy(step, spot):
            dst, device = peer(step)
            return pltpu.make_async_remote_copy(
                src_ref=buf.at[me],
                dst_ref=buf.at[spot],
                send_sem=send_sem.at[which, step],
                recv_sem=recv_sem.at[which, spot],
                device_id=device,
                device_id_type=MESH,
            )

        @pl.loop(1, devices)
        def _(step):
            copy(step, me).start()

        def wait():
            @pl.loop(1, devices)
            def _(step):
                copy(step, lax.rem(me - step + devices, devices)).wait_recv()

            @pl.loop(1, devices)
            def _(step):
                copy(step, me).wait_send()

        return wait

    def total_row(buf):
        total = buf[0]
        for spot in range(1, devices):
            total = total + buf[spot]
        return total

    def splat(row, k):
        return jnp.broadcast_to(row[:, k : k + 1], (1, LANES))

    shifts = hist_len // 2 + 1
    entry = None
    for iteration in range(iters):
        row_buf = row_bufs.at[iteration]
        moment_buf = moment_bufs.at[iteration]
        last = iteration == iters - 1

        if iteration == 0:
            loads[0].wait()
            loads[1].wait()

            def gram(step, acc):
                acc = list(acc)
                for u in range(8):
                    t = step * 8 + u
                    x = res[:, lane_tile(t)]
                    y = x * w[pl.ds(t, 1), :]
                    for r in range(shifts):
                        acc[r] = acc[r] + y * (pltpu.roll(x, r, 0) if r else x)
                return tuple(acc)

            acc = lax.fori_loop(0, tiles // 8, gram, tuple(jnp.zeros((SUBS, LANES), F32) for _ in range(shifts)))
            packed = jnp.zeros((SUBS, LANES), F32)
            for r in range(shifts):
                packed = jnp.where(lane == hist_len * r + sub, jnp.sum(acc[r], axis=1, keepdims=True), packed)
            row_buf[pl.ds(me, 1)] = (jnp.sum(packed, axis=0, keepdims=True) + slot_row)[None]
            pl.semaphore_wait(barrier, devices - 1)
        else:
            slot = slot_index[iteration - 1]
            replaced = sub == slot

            def refresh(step, acc):
                for u in range(8):
                    t = step * 8 + u
                    new_res = jnp.where(replaced, fresh[pl.ds(t, 1), :], res[:, lane_tile(t)])
                    new_rho = jnp.where(replaced, density_out[pl.ds(t, 1), :], rho[:, lane_tile(t)])
                    res[:, lane_tile(t)] = new_res
                    rho[:, lane_tile(t)] = new_rho
                    acc = acc + fresh_w[pl.ds(t, 1), :] * new_res
                return acc

            acc = lax.fori_loop(0, tiles // 8, refresh, jnp.zeros((SUBS, LANES), F32))
            packed = jnp.where(lane == sub, jnp.sum(acc, axis=1, keepdims=True), 0.0)
            row_buf[pl.ds(me, 1)] = jnp.sum(packed, axis=0, keepdims=True)[None]
        wait = exchange(row_buf, 2 * iteration)

        if iteration == 0:
            loads[2].wait()

        @pl.loop(0, rows)
        def _(r):
            xs, ys = [], []
            for q in range(4):
                b = q * rows + r
                at = pl.ds(pl.multiple_of(b * width, width), width)
                gain = jnp.concatenate([w[pl.ds(b * per_batch + v, 1), :] for v in range(per_batch)], axis=1)
                xs.extend(split(res[:, at] * gain))
                ys.append(jnp.concatenate([basis[0:24, at], jnp.broadcast_to(basis[24:25, at], (SUBS, width))], axis=0))
            x = jnp.concatenate(xs, axis=0).astype(jnp.bfloat16)
            out = None
            for y in split(jnp.concatenate(ys, axis=0)):
                part = lax.dot_general(
                    x, y.astype(jnp.bfloat16), (((1,), (1,)), ((), ())), preferred_element_type=F32
                )
                out = part if out is None else out + part
            tile = jnp.zeros((SUBS, LANES), F32)
            for q in range(4):
                block = out[24 * q : 24 * q + 8] + out[24 * q + 8 : 24 * q + 16] + out[24 * q + 16 : 24 * q + 24]
                tile = jnp.where(quarter == q, block, tile)
            hist_moments[r] = tile

        wait()

        row = total_row(row_buf)
        if iteration == 0:
            entry = [[None] * (i + 1) for i in range(hist_len)]
            for i in range(hist_len):
                for j in range(i + 1):
                    r = i - j
                    at = hist_len * r + i if r < shifts else hist_len * (hist_len - r) + j
                    entry[i][j] = splat(row, at)
        else:
            news = [splat(row, k) for k in range(hist_len)]
            slot_vec = jnp.zeros((1, LANES), jnp.int32) + slot
            entry = [
                [
                    jnp.where(slot_vec == i, news[j], jnp.where(slot_vec == j, news[i], entry[i][j]))
                    for j in range(i + 1)
                ]
                for i in range(hist_len)
            ]
        coeffs = solve_coeffs(entry, hist_len)
        coeff_col = jnp.zeros((SUBS, LANES), F32)
        for i in range(hist_len):
            coeff_col = jnp.where(sub == i, coeffs[i], coeff_col)

        mixed = [jnp.sum(coeff_col * hist_moments[r], axis=0, keepdims=True) for r in range(rows)]
        moment_buf[pl.ds(me, 1)] = jnp.concatenate(mixed, axis=0)[None]
        wait = exchange(moment_buf, 2 * iteration + 1)

        if iteration == 0:
            base = (my_member * owned).astype(F32)
            wide = lax.broadcasted_iota(jnp.int32, (owned, LANES), 0).astype(F32) + base

            @pl.loop(0, devices // SUBS)
            def _(c):
                ids = jnp.concatenate([row_buf[c * SUBS + i] for i in range(SUBS)], axis=0)
                stepped = pltpu.roll(ids, 0, 1, stride=rows, stride_axis=0)
                for q in range(4):
                    turned = pltpu.roll(stepped, (half - rows * q) % LANES, 1)
                    slots = jnp.sum(jnp.where(lane // rows == sub, turned, 0.0), axis=0, keepdims=True)
                    near[q * batches : (q + 1) * batches, lane_tile(c)] = jnp.where(
                        slot_col == slots, 1.0, 0.0
                    ).astype(jnp.bfloat16)
                    own[q * owned : (q + 1) * owned, lane_tile(c)] = jnp.where(wide == slots, 1.0, 0.0).astype(
                        jnp.bfloat16
                    )

            for load in loads[3:]:
                load.wait()

        def base_step(step, carry):
            for u in range(8):
                t = step * 8 + u
                part = coeff_col * (rho[:, lane_tile(t)] + mixing_beta * res[:, lane_tile(t)])
                base_rows[pl.ds(t, 1), :] = jnp.sum(part, axis=0, keepdims=True)
            return carry

        lax.fori_loop(0, tiles // 8, base_step, 0)
        wait()

        everywhere = moment_buf[...].reshape(devices * rows, LANES)
        pieces = jnp.concatenate([piece.astype(jnp.bfloat16) for piece in split(everywhere)], axis=1)

        def gathered(mask, count):
            out = jnp.dot(mask[...], pieces, preferred_element_type=F32)
            out = out[:, 0:LANES] + out[:, LANES : 2 * LANES] + out[:, 2 * LANES :]
            group = lax.broadcasted_iota(jnp.int32, (count, LANES), 1) // 32
            total = out[0:count]
            for q in range(1, 4):
                total = jnp.where(group == q, out[q * count : (q + 1) * count], total)
            total = total + pltpu.roll(total, 64, 1)
            total = total + pltpu.roll(total, 32, 1)
            return jnp.transpose(jnp.concatenate([total] * max(1, LANES // count), axis=0))[0:32] * scale

        at_batch = gathered(near, batches)
        comp = lax.broadcasted_iota(jnp.int32, (32, LANES), 0)
        degree = sum((comp >= (l + 1) * (l + 1)).astype(F32) for l in range(4))
        damped = jnp.where(comp < harmonics, at_batch * (mixing_beta / (1.0 + degree)), 0.0)

        def density_step(step, ahead):
            for u in range(16):
                b = step * 16 + u
                col = jnp.broadcast_to(ahead[:, u : u + 1], (32, LANES))
                for v in range(per_batch):
                    t = b * per_batch + v
                    part = col[24:32] * basis[24:25, lane_tile(t)]
                    for g in range(3):
                        part = part + col[g * SUBS : (g + 1) * SUBS] * basis[g * SUBS : (g + 1) * SUBS, lane_tile(t)]
                    correct[pl.ds(t, 1), :] = jnp.sum(part, axis=0, keepdims=True)
            return pltpu.roll(ahead, LANES - 16, 1)

        lax.fori_loop(0, batches // 16, density_step, damped)
        density = base_rows[...] - correct[...]
        density_out[...] = density
        if last:
            moments_out[...] = gathered(own, owned)[0:harmonics]
        else:
            new = target[...] + coupling[...] * jnp.tanh(density) - density
            fresh[...] = new
            fresh_w[...] = new * w[...]


def finish(density, moments, density_out, moments_out):
    density_out[...] = density[...]
    moments_out[...] = moments[...]


def local(weights, target, coupling, multipole_basis, rho_hist, res_hist, batch_atom, owner_slot, slot_index):
    harmonics, points = multipole_basis.shape
    hist_len = res_hist.shape[0]
    batches = batch_atom.shape[0]
    groups = lax.axis_size("grid")
    members = lax.axis_size("atom")
    devices = groups * members
    owned = owner_slot.shape[0] // members
    scale = 1.0 / math.sqrt(points * groups // owned)
    iters = slot_index.shape[0]
    cfg = (iters, hist_len, harmonics, batches, points // batches, owned, groups, members, scale)
    tiles = points // LANES
    flat = (tiles, LANES)
    any_space = pl.BlockSpec(memory_space=pl.ANY)
    smem = pl.BlockSpec(memory_space=pltpu.SMEM)
    vmem = pl.BlockSpec(memory_space=pltpu.VMEM)
    density, moments = pl.pallas_call(
        functools.partial(kernel, cfg),
        out_shape=(jax.ShapeDtypeStruct(flat, F32), jax.ShapeDtypeStruct((harmonics, owned), F32)),
        in_specs=[smem] * 3 + [any_space] * 6,
        out_specs=(vmem, vmem),
        scratch_shapes=[
            pltpu.VMEM(flat, F32),
            pltpu.VMEM(flat, F32),
            pltpu.VMEM(flat, F32),
            pltpu.VMEM((harmonics, points), F32),
            pltpu.VMEM((hist_len, points), F32),
            pltpu.VMEM((hist_len, points), F32),
            pltpu.VMEM(flat, F32),
            pltpu.VMEM(flat, F32),
            pltpu.VMEM((iters, devices, 1, LANES), F32),
            pltpu.VMEM((iters, devices, batches // 4, LANES), F32),
            pltpu.VMEM((4 * batches, devices * batches // 4), jnp.bfloat16),
            pltpu.VMEM((4 * owned, devices * batches // 4), jnp.bfloat16),
            pltpu.VMEM((batches // 4, SUBS, LANES), F32),
            pltpu.VMEM(flat, F32),
            pltpu.VMEM(flat, F32),
            pltpu.SemaphoreType.DMA((6,)),
            pltpu.SemaphoreType.DMA((2 * iters, devices)),
            pltpu.SemaphoreType.DMA((2 * iters, devices)),
        ],
        compiler_params=pltpu.CompilerParams(
            collective_id=0, has_side_effects=True, vmem_limit_bytes=67043328
        ),
    )(
        batch_atom,
        owner_slot,
        slot_index,
        weights.reshape(flat),
        target.reshape(flat),
        coupling.reshape(flat),
        multipole_basis,
        rho_hist,
        res_hist,
    )
    density, moments = pl.pallas_call(
        finish,
        out_shape=(jax.ShapeDtypeStruct(flat, F32), jax.ShapeDtypeStruct((harmonics, owned), F32)),
        in_specs=[vmem] * 2,
        out_specs=(vmem, vmem),
    )(density, moments)
    return density.reshape(points), moments


def solution(mesh):
    both = ("grid", "atom")
    placed = (P(both), P(both), P(both), P(None, both), P(None, both), P(None, both), P(both), P(), P())
    return jax.shard_map(
        local,
        mesh=mesh,
        in_specs=placed,
        out_specs=(P(both), P(None, "atom")),
        check_vma=False,
    )
```

profile of v0, /device:TPU:0, one launch (start us, length us, event | category | flops | bytes accessed | tf_op | source)
XLA Modules:
  0.0 40.3 jit_solution(3696675166990799315)
XLA Ops:
  0.6 38.2 %shard_map.104 = (f32[128,128]{1,0:T(8,128)}, f32[25,512]{1,0:T(8,128)}) custom-call(s32[64]{0:T(128)} %batch_atom.1, s32[2048]{0:T(1024)} %owner_slot.1, s32[2]{0:T(128)} %slot_index.1, f32[128,128]{1,0:T(8,128)} %bitcast.4, f32[128,128]{1,0:T(8,128)} %bitcast.5, f32[128,128]{1,0:T(8,128)} %bitcast.6, f32[25,16384]{1,0:T(8,128)} %basis_hbm.1, ...), custom_call_target="tpu_custom_call" | custom-call | tf_op jit(solution)/shard_map/pallas_call | solution.py:368
  38.8 1.5 %shard_map.105 = (f32[128,128]{1,0:T(8,128)}, f32[25,512]{1,0:T(8,128)}) custom-call(f32[128,128]{1,0:T(8,128)} %get-tuple-element.6.density, f32[25,512]{1,0:T(8,128)} %get-tuple-element.7.moments), custom_call_target="tpu_custom_call" | custom-call | tf_op jit(solution)/shard_map/pallas_call | solution.py:407
where the time goes:
time: 40.5 us; the launch traced here: 40.3 us
  Pallas kernels  39.7 us (98%)
  between operations  0.64 us (2%)
    pallas_call x1, Pallas kernels, local(): pl.pallas_call(functools.partial(kernel, cfg), out_shape=(jax.ShapeDtypeS...  38.2 us
    pallas_call x1, Pallas kernels, local(): pl.pallas_call(finish, out_shape=(jax.ShapeDtypeStruct(flat, F32), jax.Sh...  1.53 us

commit v1 on v0

--- a/solution.py
+++ b/solution.py
@@ -47,7 +47,7 @@
 
 def split(x):
     pieces = []
-    for _ in range(3):
+    for _ in range(2):
         piece = x.astype(jnp.bfloat16).astype(F32)
         pieces.append(piece)
         x = x - piece
@@ -56,9 +56,9 @@
 
 def kernel(
     cfg,
-    batch_atom,
-    owner_slot,
-    slot_index,
+    batch_atom_hbm,
+    owner_slot_hbm,
+    slot_index_hbm,
     w_hbm,
     target_hbm,
     coupling_hbm,
@@ -82,6 +82,9 @@
     hist_moments,
     base_rows,
     correct,
+    batch_atom,
+    owner_slot,
+    slot_index,
     load_sem,
     send_sem,
     recv_sem,
@@ -98,22 +101,37 @@
 
     def peer(step):
         spot = lax.rem(me + step, devices)
-        return spot, (lax.div(spot, members), lax.rem(spot, members))
+        return (lax.div(spot, members), lax.rem(spot, members))
 
     barrier = pltpu.get_barrier_semaphore()
-
-    @pl.loop(1, devices)
-    def _(step):
-        pl.semaphore_signal(barrier, inc=1, device_id=peer(step)[1], device_id_type=MESH)
 
     loads = [
         pltpu.make_async_copy(src, dst, load_sem.at[k])
         for k, (src, dst) in enumerate(
-            ((res_hbm, res), (w_hbm, w), (basis_hbm, basis), (rho_hbm, rho), (target_hbm, target), (coupling_hbm, coupling))
+            (
+                (res_hbm, res),
+                (w_hbm, w),
+                (basis_hbm, basis),
+                (rho_hbm, rho),
+                (target_hbm, target),
+                (coupling_hbm, coupling),
+                (batch_atom_hbm, batch_atom),
+                (owner_slot_hbm, owner_slot),
+                (slot_index_hbm, slot_index),
+            )
         )
     ]
-    for load in loads:
-        load.start()
+    for k in (6, 7, 0, 1):
+        loads[k].start()
+
+    @pl.loop(1, devices)
+    def _(step):
+        pl.semaphore_signal(barrier, inc=1, device_id=peer(step), device_id_type=MESH)
+
+    for k in (2, 3, 4, 5, 8):
+        loads[k].start()
+    loads[6].wait()
+    loads[7].wait()
 
     lane = lax.broadcasted_iota(jnp.int32, (SUBS, LANES), 1)
     sub = lax.broadcasted_iota(jnp.int32, (SUBS, LANES), 0)
@@ -136,29 +154,24 @@
         return pl.ds(pl.multiple_of(t * LANES, LANES), LANES)
 
     def exchange(buf, which):
-        def copy(step, spot):
-            dst, device = peer(step)
+        def copy(ref, step):
             return pltpu.make_async_remote_copy(
-                src_ref=buf.at[me],
-                dst_ref=buf.at[spot],
-                send_sem=send_sem.at[which, step],
-                recv_sem=recv_sem.at[which, spot],
-                device_id=device,
+                src_ref=ref,
+                dst_ref=ref,
+                send_sem=send_sem.at[which],
+                recv_sem=recv_sem.at[which],
+                device_id=peer(step),
                 device_id_type=MESH,
             )
 
         @pl.loop(1, devices)
         def _(step):
-            copy(step, me).start()
+            copy(buf.at[me], step).start()
 
         def wait():
-            @pl.loop(1, devices)
-            def _(step):
-                copy(step, lax.rem(me - step + devices, devices)).wait_recv()
-
-            @pl.loop(1, devices)
-            def _(step):
-                copy(step, me).wait_send()
+            everyone = copy(buf.at[pl.ds(0, devices - 1)], 1)
+            everyone.wait_recv()
+            everyone.wait_send()
 
         return wait
 
@@ -238,7 +251,7 @@
                 out = part if out is None else out + part
             tile = jnp.zeros((SUBS, LANES), F32)
             for q in range(4):
-                block = out[24 * q : 24 * q + 8] + out[24 * q + 8 : 24 * q + 16] + out[24 * q + 16 : 24 * q + 24]
+                block = out[16 * q : 16 * q + 8] + out[16 * q + 8 : 16 * q + 16]
                 tile = jnp.where(quarter == q, block, tile)
             hist_moments[r] = tile
 
@@ -289,8 +302,8 @@
                         jnp.bfloat16
                     )
 
-            for load in loads[3:]:
-                load.wait()
+            for k in (3, 4, 5, 8):
+                loads[k].wait()
 
         def base_step(step, carry):
             for u in range(8):
@@ -307,7 +320,7 @@
 
         def gathered(mask, count):
             out = jnp.dot(mask[...], pieces, preferred_element_type=F32)
-            out = out[:, 0:LANES] + out[:, LANES : 2 * LANES] + out[:, 2 * LANES :]
+            out = out[:, 0:LANES] + out[:, LANES:]
             group = lax.broadcasted_iota(jnp.int32, (count, LANES), 1) // 32
             total = out[0:count]
             for q in range(1, 4):
@@ -344,9 +357,15 @@
             fresh_w[...] = new * w[...]
 
 
-def finish(density, moments, density_out, moments_out):
-    density_out[...] = density[...]
-    moments_out[...] = moments[...]
+def finish(density, moments, density_out, moments_out, sem):
+    copies = [
+        pltpu.make_async_copy(density, density_out, sem.at[0]),
+        pltpu.make_async_copy(moments, moments_out, sem.at[1]),
+    ]
+    for copy in copies:
+        copy.start()
+    for copy in copies:
+        copy.wait()
 
 
 def local(weights, target, coupling, multipole_basis, rho_hist, res_hist, batch_atom, owner_slot, slot_index):
@@ -363,12 +382,11 @@
     tiles = points // LANES
     flat = (tiles, LANES)
     any_space = pl.BlockSpec(memory_space=pl.ANY)
-    smem = pl.BlockSpec(memory_space=pltpu.SMEM)
     vmem = pl.BlockSpec(memory_space=pltpu.VMEM)
     density, moments = pl.pallas_call(
         functools.partial(kernel, cfg),
         out_shape=(jax.ShapeDtypeStruct(flat, F32), jax.ShapeDtypeStruct((harmonics, owned), F32)),
-        in_specs=[smem] * 3 + [any_space] * 6,
+        in_specs=[any_space] * 9,
         out_specs=(vmem, vmem),
         scratch_shapes=[
             pltpu.VMEM(flat, F32),
@@ -386,30 +404,39 @@
             pltpu.VMEM((batches // 4, SUBS, LANES), F32),
             pltpu.VMEM(flat, F32),
             pltpu.VMEM(flat, F32),
-            pltpu.SemaphoreType.DMA((6,)),
-            pltpu.SemaphoreType.DMA((2 * iters, devices)),
-            pltpu.SemaphoreType.DMA((2 * iters, devices)),
+            pltpu.SMEM(batch_atom.shape, batch_atom.dtype),
+            pltpu.SMEM(owner_slot.shape, owner_slot.dtype),
+            pltpu.SMEM(slot_index.shape, slot_index.dtype),
+            pltpu.SemaphoreType.DMA((9,)),
+            pltpu.SemaphoreType.DMA((2 * iters,)),
+            pltpu.SemaphoreType.DMA((2 * iters,)),
         ],
         compiler_params=pltpu.CompilerParams(
-            collective_id=0, has_side_effects=True, vmem_limit_bytes=67043328
+            collective_id=0, has_side_effects=True, vmem_limit_bytes=40 * 1024 * 1024
         ),
     )(
-        batch_atom,
-        owner_slot,
-        slot_index,
-        weights.reshape(flat),
-        target.reshape(flat),
-        coupling.reshape(flat),
-        multipole_basis,
-        rho_hist,
-        res_hist,
+        *(
+            pltpu.with_memory_space_constraint(x, pltpu.HBM)
+            for x in (
+                batch_atom,
+                owner_slot,
+                slot_index,
+                weights.reshape(flat),
+                target.reshape(flat),
+                coupling.reshape(flat),
+                multipole_basis,
+                rho_hist,
+                res_hist,
+            )
+        )
     )
     density, moments = pl.pallas_call(
         finish,
         out_shape=(jax.ShapeDtypeStruct(flat, F32), jax.ShapeDtypeStruct((harmonics, owned), F32)),
         in_specs=[vmem] * 2,
-        out_specs=(vmem, vmem),
-    )(density, moments)
+        out_specs=(any_space, any_space),
+        scratch_shapes=[pltpu.SemaphoreType.DMA((2,))],
+    )(*(pltpu.with_memory_space_constraint(x, pltpu.VMEM) for x in (density, moments)))
     return density.reshape(points), moments
 
 

time: 40.5 us -> 34.4 us (0.85)
  Pallas kernels: 39.7 us -> 33.6 us
    pallas_call x1, Pallas kernels: 38.2 us -> 32.9 us  [local(): pl.pallas_call(functools.partial(kernel, cfg), out_shape=(jax.ShapeDtypeS...]
    pallas_call x1, Pallas kernels: 1.53 us -> 0.67 us  [local(): pl.pallas_call(finish, out_shape=(jax.ShapeDtypeStruct(flat, F32), jax.Sh...]
where the time goes in v1:
time: 34.4 us; the launch traced here: 34.2 us
  Pallas kernels  33.6 us (98%)
  between operations  0.64 us (2%)
    pallas_call x1, Pallas kernels, local(): pl.pallas_call(functools.partial(kernel, cfg), out_shape=(jax.ShapeDtypeS...  32.9 us

profile of v1, /device:TPU:0, one launch (start us, length us, event | category | flops | bytes accessed | tf_op | source)
XLA Modules:
  0.0 34.2 jit_solution(12141546891704013198)
XLA Ops:
  0.6 32.9 %shard_map.104 = (f32[128,128]{1,0:T(8,128)S(1)}, f32[25,512]{1,0:T(8,128)S(1)}) custom-call(s32[64]{0:T(128)} %batch_atom_hbm.1, s32[2048]{0:T(1024)} %owner_slot_hbm.1, s32[2]{0:T(128)} %slot_index_hbm.1, f32[128,128]{1,0:T(8,128)} %bitcast.4, f32[128,128]{1,0:T(8,128)} %bitcast.5, f32[128,128]{1,0:T(8,128)} %bitcast.6, f32[25,16384]{1,0:T(8,128)} %basis_hbm.1, ...), custom_call_target="tpu_custom_call" | custom-call | tf_op jit(solution)/shard_map/pallas_call | solution.py:386
  33.6 0.7 %shard_map.105 = (f32[128,128]{1,0:T(8,128)}, f32[25,512]{1,0:T(8,128)}) custom-call(f32[128,128]{1,0:T(8,128)S(1)} %get-tuple-element.6.density, f32[25,512]{1,0:T(8,128)S(1)} %get-tuple-element.7.moments), custom_call_target="tpu_custom_call" | custom-call | tf_op jit(solution)/shard_map/pallas_call | solution.py:433

commit v2 on v1

--- a/solution.py
+++ b/solution.py
@@ -54,6 +54,39 @@
     return pieces
 
 
+def flips(value, count):
+    out = []
+    bit = 1
+    while bit < count:
+        out.append(bit - 2 * bit * lax.rem(lax.div(value, bit), 2))
+        bit *= 2
+    return out
+
+
+def flipped(value, changes, mask):
+    for k, change in enumerate(changes):
+        if mask >> k & 1:
+            value = value + change
+    return value
+
+
+def stacked_sums(parts, sub):
+    low = sub % 8 < 4
+    halves = [
+        jnp.where(low, parts[t], parts[t + 4]) + pltpu.roll(jnp.where(low, parts[t + 4], parts[t]), 4, 0)
+        for t in range(4)
+    ]
+    low = sub % 4 < 2
+    quarters = [
+        jnp.where(low, halves[t] + pltpu.roll(halves[t], 6, 0), halves[t + 2] + pltpu.roll(halves[t + 2], 2, 0))
+        for t in range(2)
+    ]
+    low = sub % 2 < 1
+    return jnp.where(
+        low, quarters[0] + pltpu.roll(quarters[0], 7, 0), quarters[1] + pltpu.roll(quarters[1], 1, 0)
+    )
+
+
 def kernel(
     cfg,
     batch_atom_hbm,
@@ -76,9 +109,11 @@
     fresh,
     fresh_w,
     row_bufs,
-    moment_bufs,
+    sent_moments,
+    all_moments,
     near,
     own,
+    own_sum,
     hist_moments,
     base_rows,
     correct,
@@ -86,8 +121,8 @@
     owner_slot,
     slot_index,
     load_sem,
-    send_sem,
-    recv_sem,
+    row_sem,
+    moment_sem,
 ):
     iters, hist_len, harmonics, batches, width, owned, groups, members, scale = cfg
     devices = groups * members
@@ -98,10 +133,22 @@
     my_group = lax.axis_index("grid")
     my_member = lax.axis_index("atom")
     me = my_group * members + my_member
+    chips = devices // 2
+    upper = chips // 2
+    chip = lax.div(me, 2)
+    core = lax.rem(me, 2)
+    group_flips = flips(my_group, groups)
+    member_flips = flips(my_member, members)
 
     def peer(step):
-        spot = lax.rem(me + step, devices)
-        return (lax.div(spot, members), lax.rem(spot, members))
+        return (
+            flipped(my_group, group_flips, step // members),
+            flipped(my_member, member_flips, step % members),
+        )
+
+    plane = min(chips, (members // 2) ** 2)
+    chip_steps = [z * plane + p for p in reversed(range(plane)) for z in reversed(range(chips // plane))]
+    device_steps = [2 * step + c for step in chip_steps for c in (1, 0)][:-1]
 
     barrier = pltpu.get_barrier_semaphore()
 
@@ -124,8 +171,7 @@
     for k in (6, 7, 0, 1):
         loads[k].start()
 
-    @pl.loop(1, devices)
-    def _(step):
+    for step in device_steps:
         pl.semaphore_signal(barrier, inc=1, device_id=peer(step), device_id_type=MESH)
 
     for k in (2, 3, 4, 5, 8):
@@ -153,27 +199,49 @@
     def lane_tile(t):
         return pl.ds(pl.multiple_of(t * LANES, LANES), LANES)
 
-    def exchange(buf, which):
-        def copy(ref, step):
-            return pltpu.make_async_remote_copy(
-                src_ref=ref,
-                dst_ref=ref,
-                send_sem=send_sem.at[which],
-                recv_sem=recv_sem.at[which],
-                device_id=peer(step),
-                device_id_type=MESH,
-            )
-
-        @pl.loop(1, devices)
-        def _(step):
-            copy(buf.at[me], step).start()
+    def remote(src, dst, sems, step):
+        return pltpu.make_async_remote_copy(
+            src_ref=src,
+            dst_ref=dst,
+            send_sem=sems.at[0],
+            recv_sem=sems.at[1],
+            device_id=peer(step),
+            device_id_type=MESH,
+        )
+
+    def exchange_rows(buf, sems):
+        for step in device_steps:
+            remote(buf.at[me], buf.at[me], sems, step).start()
 
         def wait():
-            everyone = copy(buf.at[pl.ds(0, devices - 1)], 1)
+            others = buf.at[pl.ds(0, devices - 1)]
+            everyone = remote(others, others, sems, 1)
             everyone.wait_recv()
             everyone.wait_send()
 
         return wait
+
+    def exchange_moments(mine, buf, sems):
+        halves = [pl.ds((upper * k + chip - lax.rem(chip, upper)) % chips, upper) for k in range(2)]
+        remote(mine, buf.at[0, chip], sems.at[0], 1).start()
+        for step in chip_steps[:-1]:
+            remote(mine, buf.at[0, chip], sems.at[step // upper], 2 * step + 1).start()
+        landed = [remote(buf.at[0, half], buf.at[0, half], sems.at[k], 1) for k, half in enumerate(halves)]
+        passed = [remote(buf.at[0, half], buf.at[1, half], sems.at[2 + k], 1) for k, half in enumerate(halves)]
+
+        def wait_landed():
+            for k in range(2):
+                landed[k].wait_recv()
+                passed[k].start()
+
+        def wait_passed():
+            for k in range(2):
+                passed[k].wait_recv()
+            for k in range(2):
+                landed[k].wait_send()
+                passed[k].wait_send()
+
+        return wait_landed, wait_passed
 
     def total_row(buf):
         total = buf[0]
@@ -188,7 +256,8 @@
     entry = None
     for iteration in range(iters):
         row_buf = row_bufs.at[iteration]
-        moment_buf = moment_bufs.at[iteration]
+        sent_buf = sent_moments.at[iteration]
+        moment_buf = all_moments.at[iteration]
         last = iteration == iters - 1
 
         if iteration == 0:
@@ -215,23 +284,30 @@
             slot = slot_index[iteration - 1]
             replaced = sub == slot
 
-            def refresh(step, acc):
+            def inner(step, acc):
+                acc = list(acc)
+                for u in range(16):
+                    t = step * 16 + u
+                    acc[u % 4] = acc[u % 4] + fresh_w[pl.ds(t, 1), :] * res[:, lane_tile(t)]
+                return tuple(acc)
+
+            acc = lax.fori_loop(0, tiles // 16, inner, tuple(jnp.zeros((SUBS, LANES), F32) for _ in range(4)))
+            acc = (acc[0] + acc[1]) + (acc[2] + acc[3])
+            acc = jnp.where(replaced, square, acc)
+            packed = jnp.where(lane == sub, jnp.sum(acc, axis=1, keepdims=True), 0.0)
+            row_buf[pl.ds(me, 1)] = jnp.sum(packed, axis=0, keepdims=True)[None]
+        wait = exchange_rows(row_buf, row_sem.at[iteration])
+
+        if iteration == 0:
+            loads[2].wait()
+        else:
+
+            @pl.loop(0, tiles // 8)
+            def _(step):
                 for u in range(8):
                     t = step * 8 + u
-                    new_res = jnp.where(replaced, fresh[pl.ds(t, 1), :], res[:, lane_tile(t)])
-                    new_rho = jnp.where(replaced, density_out[pl.ds(t, 1), :], rho[:, lane_tile(t)])
-                    res[:, lane_tile(t)] = new_res
-                    rho[:, lane_tile(t)] = new_rho
-                    acc = acc + fresh_w[pl.ds(t, 1), :] * new_res
-                return acc
-
-            acc = lax.fori_loop(0, tiles // 8, refresh, jnp.zeros((SUBS, LANES), F32))
-            packed = jnp.where(lane == sub, jnp.sum(acc, axis=1, keepdims=True), 0.0)
-            row_buf[pl.ds(me, 1)] = jnp.sum(packed, axis=0, keepdims=True)[None]
-        wait = exchange(row_buf, 2 * iteration)
-
-        if iteration == 0:
-            loads[2].wait()
+                    res[:, lane_tile(t)] = jnp.where(replaced, fresh[pl.ds(t, 1), :], res[:, lane_tile(t)])
+                    rho[:, lane_tile(t)] = jnp.where(replaced, density_out[pl.ds(t, 1), :], rho[:, lane_tile(t)])
 
         @pl.loop(0, rows)
         def _(r):
@@ -281,8 +357,8 @@
             coeff_col = jnp.where(sub == i, coeffs[i], coeff_col)
 
         mixed = [jnp.sum(coeff_col * hist_moments[r], axis=0, keepdims=True) for r in range(rows)]
-        moment_buf[pl.ds(me, 1)] = jnp.concatenate(mixed, axis=0)[None]
-        wait = exchange(moment_buf, 2 * iteration + 1)
+        sent_buf[...] = jnp.concatenate(mixed, axis=0)
+        wait_landed, wait_passed = exchange_moments(sent_buf, moment_buf, moment_sem.at[iteration])
 
         if iteration == 0:
             base = (my_member * owned).astype(F32)
@@ -290,7 +366,9 @@
 
             @pl.loop(0, devices // SUBS)
             def _(c):
-                ids = jnp.concatenate([row_buf[c * SUBS + i] for i in range(SUBS)], axis=0)
+                side = lax.div(c, chips // SUBS)
+                first = 2 * SUBS * lax.rem(c, chips // SUBS) + lax.rem(core + 1 + side, 2)
+                ids = jnp.concatenate([row_buf[first + 2 * i] for i in range(SUBS)], axis=0)
                 stepped = pltpu.roll(ids, 0, 1, stride=rows, stride_axis=0)
                 for q in range(4):
                     turned = pltpu.roll(stepped, (half - rows * q) % LANES, 1)
@@ -313,48 +391,60 @@
             return carry
 
         lax.fori_loop(0, tiles // 8, base_step, 0)
-        wait()
-
-        everywhere = moment_buf[...].reshape(devices * rows, LANES)
-        pieces = jnp.concatenate([piece.astype(jnp.bfloat16) for piece in split(everywhere)], axis=1)
-
-        def gathered(mask, count):
-            out = jnp.dot(mask[...], pieces, preferred_element_type=F32)
+        depth = chips * rows
+
+        def gathered(mask, count, side):
+            everywhere = moment_buf[side].reshape(depth, LANES)
+            pieces = jnp.concatenate([piece.astype(jnp.bfloat16) for piece in split(everywhere)], axis=1)
+            out = jnp.dot(mask[:, side * depth : (side + 1) * depth], pieces, preferred_element_type=F32)
             out = out[:, 0:LANES] + out[:, LANES:]
             group = lax.broadcasted_iota(jnp.int32, (count, LANES), 1) // 32
             total = out[0:count]
             for q in range(1, 4):
                 total = jnp.where(group == q, out[q * count : (q + 1) * count], total)
+            return total
+
+        def folded(total, count):
             total = total + pltpu.roll(total, 64, 1)
             total = total + pltpu.roll(total, 32, 1)
             return jnp.transpose(jnp.concatenate([total] * max(1, LANES // count), axis=0))[0:32] * scale
 
-        at_batch = gathered(near, batches)
+        wait_landed()
+        near_sum = gathered(near, batches, 0)
+        if last:
+            own_sum[...] = gathered(own, owned, 0)
+        wait_passed()
+        at_batch = folded(near_sum + gathered(near, batches, 1), batches)
+        if last:
+            moments_out[...] = folded(own_sum[...] + gathered(own, owned, 1), owned)[0:harmonics]
         comp = lax.broadcasted_iota(jnp.int32, (32, LANES), 0)
         degree = sum((comp >= (l + 1) * (l + 1)).astype(F32) for l in range(4))
         damped = jnp.where(comp < harmonics, at_batch * (mixing_beta / (1.0 + degree)), 0.0)
 
         def density_step(step, ahead):
-            for u in range(16):
-                b = step * 16 + u
-                col = jnp.broadcast_to(ahead[:, u : u + 1], (32, LANES))
-                for v in range(per_batch):
-                    t = b * per_batch + v
-                    part = col[24:32] * basis[24:25, lane_tile(t)]
-                    for g in range(3):
-                        part = part + col[g * SUBS : (g + 1) * SUBS] * basis[g * SUBS : (g + 1) * SUBS, lane_tile(t)]
-                    correct[pl.ds(t, 1), :] = jnp.sum(part, axis=0, keepdims=True)
+            for base in range(0, 16, SUBS // per_batch):
+                parts = []
+                for u in range(base, base + SUBS // per_batch):
+                    col = jnp.broadcast_to(ahead[:, u : u + 1], (32, LANES))
+                    for v in range(per_batch):
+                        at = lane_tile((step * 16 + u) * per_batch + v)
+                        part = col[24:32] * basis[24:25, at]
+                        for g in range(3):
+                            part = part + col[g * SUBS : (g + 1) * SUBS] * basis[g * SUBS : (g + 1) * SUBS, at]
+                        parts.append(part)
+                at = pl.multiple_of((step * 16 + base) * per_batch, SUBS)
+                correct[pl.ds(at, SUBS), :] = stacked_sums(parts, sub)
             return pltpu.roll(ahead, LANES - 16, 1)
 
         lax.fori_loop(0, batches // 16, density_step, damped)
         density = base_rows[...] - correct[...]
         density_out[...] = density
-        if last:
-            moments_out[...] = gathered(own, owned)[0:harmonics]
-        else:
+        if not last:
             new = target[...] + coupling[...] * jnp.tanh(density) - density
+            new_w = new * w[...]
             fresh[...] = new
-            fresh_w[...] = new * w[...]
+            fresh_w[...] = new_w
+            square = jnp.sum(new * new_w, axis=0, keepdims=True)
 
 
 def finish(density, moments, density_out, moments_out, sem):
@@ -398,9 +488,11 @@
             pltpu.VMEM(flat, F32),
             pltpu.VMEM(flat, F32),
             pltpu.VMEM((iters, devices, 1, LANES), F32),
-            pltpu.VMEM((iters, devices, batches // 4, LANES), F32),
+            pltpu.VMEM((iters, batches // 4, LANES), F32),
+            pltpu.VMEM((iters, 2, devices // 2, batches // 4, LANES), F32),
             pltpu.VMEM((4 * batches, devices * batches // 4), jnp.bfloat16),
             pltpu.VMEM((4 * owned, devices * batches // 4), jnp.bfloat16),
+            pltpu.VMEM((owned, LANES), F32),
             pltpu.VMEM((batches // 4, SUBS, LANES), F32),
             pltpu.VMEM(flat, F32),
             pltpu.VMEM(flat, F32),
@@ -408,8 +500,8 @@
             pltpu.SMEM(owner_slot.shape, owner_slot.dtype),
             pltpu.SMEM(slot_index.shape, slot_index.dtype),
             pltpu.SemaphoreType.DMA((9,)),
-            pltpu.SemaphoreType.DMA((2 * iters,)),
-            pltpu.SemaphoreType.DMA((2 * iters,)),
+            pltpu.SemaphoreType.DMA((iters, 2)),
+            pltpu.SemaphoreType.DMA((iters, 4, 2)),
         ],
         compiler_params=pltpu.CompilerParams(
             collective_id=0, has_side_effects=True, vmem_limit_bytes=40 * 1024 * 1024

time: 34.4 us -> 31.6 us (0.919)
  Pallas kernels: 33.6 us -> 30.8 us
    pallas_call x1, Pallas kernels: 32.9 us -> 30.1 us  [local(): pl.pallas_call(functools.partial(kernel, cfg), out_shape=(jax.ShapeDtypeS...]
where the time goes in v2:
time: 31.6 us; the launch traced here: 31.4 us
  Pallas kernels  30.8 us (97%)
  between operations  0.64 us (2%)
    pallas_call x1, Pallas kernels, local(): pl.pallas_call(functools.partial(kernel, cfg), out_shape=(jax.ShapeDtypeS...  30.1 us
    pallas_call x1, Pallas kernels, local(): pl.pallas_call(finish, out_shape=(jax.ShapeDtypeStruct(flat, F32), jax.Sh...  0.67 us

profile of v2, /device:TPU:0, one launch (start us, length us, event | category | flops | bytes accessed | tf_op | source)
XLA Modules:
  0.0 31.4 jit_solution(8845400061727058087)
XLA Ops:
  0.6 30.1 %shard_map.104 = (f32[128,128]{1,0:T(8,128)S(1)}, f32[25,512]{1,0:T(8,128)S(1)}) custom-call(s32[64]{0:T(128)} %batch_atom_hbm.1, s32[2048]{0:T(1024)} %owner_slot_hbm.1, s32[2]{0:T(128)} %slot_index_hbm.1, f32[128,128]{1,0:T(8,128)} %bitcast.4, f32[128,128]{1,0:T(8,128)} %bitcast.5, f32[128,128]{1,0:T(8,128)} %bitcast.6, f32[25,16384]{1,0:T(8,128)} %basis_hbm.1, ...), custom_call_target="tpu_custom_call" | custom-call | tf_op jit(solution)/shard_map/pallas_call | solution.py:476
  30.8 0.7 %shard_map.105 = (f32[128,128]{1,0:T(8,128)}, f32[25,512]{1,0:T(8,128)}) custom-call(f32[128,128]{1,0:T(8,128)S(1)} %get-tuple-element.6.density, f32[25,512]{1,0:T(8,128)S(1)} %get-tuple-element.7.moments), custom_call_target="tpu_custom_call" | custom-call | tf_op jit(solution)/shard_map/pallas_call | solution.py:525

commit v3 on v2

--- a/solution.py
+++ b/solution.py
@@ -70,23 +70,6 @@
     return value
 
 
-def stacked_sums(parts, sub):
-    low = sub % 8 < 4
-    halves = [
-        jnp.where(low, parts[t], parts[t + 4]) + pltpu.roll(jnp.where(low, parts[t + 4], parts[t]), 4, 0)
-        for t in range(4)
-    ]
-    low = sub % 4 < 2
-    quarters = [
-        jnp.where(low, halves[t] + pltpu.roll(halves[t], 6, 0), halves[t + 2] + pltpu.roll(halves[t + 2], 2, 0))
-        for t in range(2)
-    ]
-    low = sub % 2 < 1
-    return jnp.where(
-        low, quarters[0] + pltpu.roll(quarters[0], 7, 0), quarters[1] + pltpu.roll(quarters[1], 1, 0)
-    )
-
-
 def kernel(
     cfg,
     batch_atom_hbm,
@@ -114,6 +97,7 @@
     near,
     own,
     own_sum,
+    halves,
     hist_moments,
     base_rows,
     correct,
@@ -244,10 +228,10 @@
         return wait_landed, wait_passed
 
     def total_row(buf):
-        total = buf[0]
-        for spot in range(1, devices):
-            total = total + buf[spot]
-        return total
+        parts = [buf[spot] for spot in range(devices)]
+        while len(parts) > 1:
+            parts = [parts[k] + parts[k + 1] for k in range(0, len(parts), 2)]
+        return parts[0]
 
     def splat(row, k):
         return jnp.broadcast_to(row[:, k : k + 1], (1, LANES))
@@ -284,14 +268,9 @@
             slot = slot_index[iteration - 1]
             replaced = sub == slot
 
-            def inner(step, acc):
-                acc = list(acc)
-                for u in range(16):
-                    t = step * 16 + u
-                    acc[u % 4] = acc[u % 4] + fresh_w[pl.ds(t, 1), :] * res[:, lane_tile(t)]
-                return tuple(acc)
-
-            acc = lax.fori_loop(0, tiles // 16, inner, tuple(jnp.zeros((SUBS, LANES), F32) for _ in range(4)))
+            acc = [jnp.zeros((SUBS, LANES), F32) for _ in range(4)]
+            for t in range(tiles):
+                acc[t % 4] = acc[t % 4] + fresh_w[t : t + 1, :] * res[:, t * LANES : (t + 1) * LANES]
             acc = (acc[0] + acc[1]) + (acc[2] + acc[3])
             acc = jnp.where(replaced, square, acc)
             packed = jnp.where(lane == sub, jnp.sum(acc, axis=1, keepdims=True), 0.0)
@@ -317,13 +296,20 @@
                 at = pl.ds(pl.multiple_of(b * width, width), width)
                 gain = jnp.concatenate([w[pl.ds(b * per_batch + v, 1), :] for v in range(per_batch)], axis=1)
                 xs.extend(split(res[:, at] * gain))
-                ys.append(jnp.concatenate([basis[0:24, at], jnp.broadcast_to(basis[24:25, at], (SUBS, width))], axis=0))
+                slab = pl.ds(pl.multiple_of(b * 32, 32), 32)
+                if iteration == 0:
+                    y = jnp.concatenate([basis[0:24, at], jnp.broadcast_to(basis[24:25, at], (SUBS, width))], axis=0)
+                    pair = [piece.astype(jnp.bfloat16) for piece in split(y)]
+                    for k in range(2):
+                        halves[k, slab, :] = pair[k]
+                else:
+                    pair = [halves[k, slab, :] for k in range(2)]
+                ys.append(pair)
             x = jnp.concatenate(xs, axis=0).astype(jnp.bfloat16)
             out = None
-            for y in split(jnp.concatenate(ys, axis=0)):
-                part = lax.dot_general(
-                    x, y.astype(jnp.bfloat16), (((1,), (1,)), ((), ())), preferred_element_type=F32
-                )
+            for k in range(2):
+                y = jnp.concatenate([pair[k] for pair in ys], axis=0)
+                part = lax.dot_general(x, y, (((1,), (1,)), ((), ())), preferred_element_type=F32)
                 out = part if out is None else out + part
             tile = jnp.zeros((SUBS, LANES), F32)
             for q in range(4):
@@ -404,41 +390,45 @@
                 total = jnp.where(group == q, out[q * count : (q + 1) * count], total)
             return total
 
-        def folded(total, count):
+        def folded(total):
             total = total + pltpu.roll(total, 64, 1)
-            total = total + pltpu.roll(total, 32, 1)
-            return jnp.transpose(jnp.concatenate([total] * max(1, LANES // count), axis=0))[0:32] * scale
+            return (total + pltpu.roll(total, 32, 1)) * scale
 
         wait_landed()
         near_sum = gathered(near, batches, 0)
         if last:
             own_sum[...] = gathered(own, owned, 0)
         wait_passed()
-        at_batch = folded(near_sum + gathered(near, batches, 1), batches)
+        near_sum = near_sum + gathered(near, batches, 1)
         if last:
-            moments_out[...] = folded(own_sum[...] + gathered(own, owned, 1), owned)[0:harmonics]
-        comp = lax.broadcasted_iota(jnp.int32, (32, LANES), 0)
+            own_sum[...] = own_sum[...] + gathered(own, owned, 1)
+        at_batch = folded(near_sum)
+        comp = lax.broadcasted_iota(jnp.int32, (batches, LANES), 1) % 32
+        spot = lax.broadcasted_iota(jnp.int32, (batches, LANES), 0) % SUBS
+        turn = lax.broadcasted_iota(jnp.int32, (batches, LANES), 1) // 32
         degree = sum((comp >= (l + 1) * (l + 1)).astype(F32) for l in range(4))
         damped = jnp.where(comp < harmonics, at_batch * (mixing_beta / (1.0 + degree)), 0.0)
-
-        def density_step(step, ahead):
-            for base in range(0, 16, SUBS // per_batch):
-                parts = []
-                for u in range(base, base + SUBS // per_batch):
-                    col = jnp.broadcast_to(ahead[:, u : u + 1], (32, LANES))
-                    for v in range(per_batch):
-                        at = lane_tile((step * 16 + u) * per_batch + v)
-                        part = col[24:32] * basis[24:25, at]
-                        for g in range(3):
-                            part = part + col[g * SUBS : (g + 1) * SUBS] * basis[g * SUBS : (g + 1) * SUBS, at]
-                        parts.append(part)
-                at = pl.multiple_of((step * 16 + base) * per_batch, SUBS)
-                correct[pl.ds(at, SUBS), :] = stacked_sums(parts, sub)
-            return pltpu.roll(ahead, LANES - 16, 1)
-
-        lax.fori_loop(0, batches // 16, density_step, damped)
+        spread = jnp.concatenate([jnp.where(spot == turn + 4 * side, damped, 0.0) for side in range(2)], axis=1)
+        high, low = split(spread)
+        for g in range(batches // SUBS):
+            mine = slice(g * SUBS, (g + 1) * SUBS)
+            x = jnp.concatenate([high[mine], low[mine]], axis=0).astype(jnp.bfloat16)
+            out = None
+            for k in range(2):
+                y = halves[k, g * SUBS * 32 : (g + 1) * SUBS * 32, :]
+                part = jnp.dot(x, y, preferred_element_type=F32)
+                out = part if out is None else out + part
+            out = out[0:SUBS] + out[SUBS:]
+            for v in range(per_batch):
+                correct[pl.ds(g * SUBS * per_batch + v, SUBS, stride=per_batch), :] = out[
+                    :, v * LANES : (v + 1) * LANES
+                ]
         density = base_rows[...] - correct[...]
         density_out[...] = density
+        if last:
+            turned = jnp.transpose(own_sum[...])
+            final = (turned[0:32] + turned[32:64]) + (turned[64:96] + turned[96:128])
+            moments_out[...] = final[0:harmonics] * scale
         if not last:
             new = target[...] + coupling[...] * jnp.tanh(density) - density
             new_w = new * w[...]
@@ -493,6 +483,7 @@
             pltpu.VMEM((4 * batches, devices * batches // 4), jnp.bfloat16),
             pltpu.VMEM((4 * owned, devices * batches // 4), jnp.bfloat16),
             pltpu.VMEM((owned, LANES), F32),
+            pltpu.VMEM((2, batches * 32, points // batches), jnp.bfloat16),
             pltpu.VMEM((batches // 4, SUBS, LANES), F32),
             pltpu.VMEM(flat, F32),
             pltpu.VMEM(flat, F32),

time: 31.6 us -> 30.2 us (0.956)
  Pallas kernels: 30.8 us -> 29.4 us
    pallas_call x1, Pallas kernels: 30.1 us -> 28.7 us  [local(): pl.pallas_call(functools.partial(kernel, cfg), out_shape=(jax.ShapeDtypeS...]
where the time goes in v3:
time: 30.2 us; the launch traced here: 30.1 us
  Pallas kernels  29.4 us (97%)
  between operations  0.64 us (2%)
    pallas_call x1, Pallas kernels, local(): pl.pallas_call(functools.partial(kernel, cfg), out_shape=(jax.ShapeDtypeS...  28.7 us
    pallas_call x1, Pallas kernels, local(): pl.pallas_call(finish, out_shape=(jax.ShapeDtypeStruct(flat, F32), jax.Sh...  0.67 us

profile of v3, /device:TPU:0, one launch (start us, length us, event | category | flops | bytes accessed | tf_op | source)
XLA Modules:
  0.0 30.1 jit_solution(12811255011535327416)
XLA Ops:
  0.6 28.7 %shard_map.104 = (f32[128,128]{1,0:T(8,128)S(1)}, f32[25,512]{1,0:T(8,128)S(1)}) custom-call(s32[64]{0:T(128)} %batch_atom_hbm.1, s32[2048]{0:T(1024)} %owner_slot_hbm.1, s32[2]{0:T(128)} %slot_index_hbm.1, f32[128,128]{1,0:T(8,128)} %bitcast.4, f32[128,128]{1,0:T(8,128)} %bitcast.5, f32[128,128]{1,0:T(8,128)} %bitcast.6, f32[25,16384]{1,0:T(8,128)} %basis_hbm.1, ...), custom_call_target="tpu_custom_call" | custom-call | tf_op jit(solution)/shard_map/pallas_call | solution.py:466
  29.4 0.7 %shard_map.105 = (f32[128,128]{1,0:T(8,128)}, f32[25,512]{1,0:T(8,128)}) custom-call(f32[128,128]{1,0:T(8,128)S(1)} %get-tuple-element.6.density, f32[25,512]{1,0:T(8,128)S(1)} %get-tuple-element.7.moments), custom_call_target="tpu_custom_call" | custom-call | tf_op jit(solution)/shard_map/pallas_call | solution.py:516

commit v4 on v3

--- a/solution.py
+++ b/solution.py
@@ -205,11 +205,27 @@
 
         return wait
 
-    def exchange_moments(mine, buf, sems):
+    def exchange_moments(mine, buf, sems, favour):
         halves = [pl.ds((upper * k + chip - lax.rem(chip, upper)) % chips, upper) for k in range(2)]
         remote(mine, buf.at[0, chip], sems.at[0], 1).start()
-        for step in chip_steps[:-1]:
+        def send(step):
             remote(mine, buf.at[0, chip], sems.at[step // upper], 2 * step + 1).start()
+
+        if favour:
+            origin = pltpu.make_async_remote_copy(
+                src_ref=mine,
+                dst_ref=buf.at[0, chip],
+                send_sem=sems.at[lax.div(chip, upper), 0],
+                recv_sem=sems.at[lax.div(chip, upper), 1],
+                device_id=(0, 1 - core),
+                device_id_type=MESH,
+            )
+            pl.when(chip != 0)(origin.start)
+            for step in chip_steps[:-1]:
+                pl.when(chip != step)(functools.partial(send, step))
+        else:
+            for step in chip_steps[:-1]:
+                send(step)
         landed = [remote(buf.at[0, half], buf.at[0, half], sems.at[k], 1) for k, half in enumerate(halves)]
         passed = [remote(buf.at[0, half], buf.at[1, half], sems.at[2 + k], 1) for k, half in enumerate(halves)]
 
@@ -344,7 +360,7 @@
 
         mixed = [jnp.sum(coeff_col * hist_moments[r], axis=0, keepdims=True) for r in range(rows)]
         sent_buf[...] = jnp.concatenate(mixed, axis=0)
-        wait_landed, wait_passed = exchange_moments(sent_buf, moment_buf, moment_sem.at[iteration])
+        wait_landed, wait_passed = exchange_moments(sent_buf, moment_buf, moment_sem.at[iteration], last)
 
         if iteration == 0:
             base = (my_member * owned).astype(F32)
@@ -362,9 +378,7 @@
                     near[q * batches : (q + 1) * batches, lane_tile(c)] = jnp.where(
                         slot_col == slots, 1.0, 0.0
                     ).astype(jnp.bfloat16)
-                    own[q * owned : (q + 1) * owned, lane_tile(c)] = jnp.where(wide == slots, 1.0, 0.0).astype(
-                        jnp.bfloat16
-                    )
+                    own[:, lane_tile(4 * c + q)] = jnp.where(wide == slots, 1.0, 0.0).astype(jnp.bfloat16)
 
             for k in (3, 4, 5, 8):
                 loads[k].wait()
@@ -379,29 +393,46 @@
         lax.fori_loop(0, tiles // 8, base_step, 0)
         depth = chips * rows
 
-        def gathered(mask, count, side):
+        def pieces_of(side):
             everywhere = moment_buf[side].reshape(depth, LANES)
-            pieces = jnp.concatenate([piece.astype(jnp.bfloat16) for piece in split(everywhere)], axis=1)
-            out = jnp.dot(mask[:, side * depth : (side + 1) * depth], pieces, preferred_element_type=F32)
+            return jnp.concatenate([piece.astype(jnp.bfloat16) for piece in split(everywhere)], axis=1)
+
+        def near_part(pieces, side):
+            out = jnp.dot(near[:, side * depth : (side + 1) * depth], pieces, preferred_element_type=F32)
             out = out[:, 0:LANES] + out[:, LANES:]
-            group = lax.broadcasted_iota(jnp.int32, (count, LANES), 1) // 32
-            total = out[0:count]
+            group = lax.broadcasted_iota(jnp.int32, (batches, LANES), 1) // 32
+            total = out[0:batches]
             for q in range(1, 4):
-                total = jnp.where(group == q, out[q * count : (q + 1) * count], total)
+                total = jnp.where(group == q, out[q * batches : (q + 1) * batches], total)
             return total
+
+        def own_part(pieces, side):
+            turn = lax.broadcasted_iota(jnp.int32, (1, 2 * LANES), 1) % LANES // 32
+            picks = [jnp.where(turn == q, 1.0, 0.0).astype(jnp.bfloat16) for q in range(4)]
+            stacked = jnp.concatenate(
+                [pieces[c : c + LANES] * pick for c in range(0, depth, LANES) for pick in picks], axis=0
+            )
+            outs = []
+            for k in range(2):
+                mine = own[k * owned // 2 : (k + 1) * owned // 2, 4 * side * depth : 4 * (side + 1) * depth]
+                out = jnp.dot(mine, stacked, preferred_element_type=F32)
+                outs.append(out[:, 0:LANES] + out[:, LANES:])
+            return jnp.concatenate(outs, axis=0)
 
         def folded(total):
             total = total + pltpu.roll(total, 64, 1)
             return (total + pltpu.roll(total, 32, 1)) * scale
 
         wait_landed()
-        near_sum = gathered(near, batches, 0)
+        pieces = pieces_of(0)
+        near_sum = near_part(pieces, 0)
         if last:
-            own_sum[...] = gathered(own, owned, 0)
+            own_sum[...] = own_part(pieces, 0)
         wait_passed()
-        near_sum = near_sum + gathered(near, batches, 1)
+        pieces = pieces_of(1)
+        near_sum = near_sum + near_part(pieces, 1)
         if last:
-            own_sum[...] = own_sum[...] + gathered(own, owned, 1)
+            own_sum[...] = own_sum[...] + own_part(pieces, 1)
         at_batch = folded(near_sum)
         comp = lax.broadcasted_iota(jnp.int32, (batches, LANES), 1) % 32
         spot = lax.broadcasted_iota(jnp.int32, (batches, LANES), 0) % SUBS
@@ -481,7 +512,7 @@
             pltpu.VMEM((iters, batches // 4, LANES), F32),
             pltpu.VMEM((iters, 2, devices // 2, batches // 4, LANES), F32),
             pltpu.VMEM((4 * batches, devices * batches // 4), jnp.bfloat16),
-            pltpu.VMEM((4 * owned, devices * batches // 4), jnp.bfloat16),
+            pltpu.VMEM((owned, devices * batches), jnp.bfloat16),
             pltpu.VMEM((owned, LANES), F32),
             pltpu.VMEM((2, batches * 32, points // batches), jnp.bfloat16),
             pltpu.VMEM((batches // 4, SUBS, LANES), F32),

time: 30.2 us -> 29.7 us (0.983)
  Pallas kernels: 29.4 us -> 28.9 us
    pallas_call x1, Pallas kernels: 28.7 us -> 28.2 us  [local(): pl.pallas_call(functools.partial(kernel, cfg), out_shape=(jax.ShapeDtypeS...]
where the time goes in v4:
time: 29.7 us; the launch traced here: 29.5 us
  Pallas kernels  28.9 us (97%)
  between operations  0.64 us (2%)
    pallas_call x1, Pallas kernels, local(): pl.pallas_call(functools.partial(kernel, cfg), out_shape=(jax.ShapeDtypeS...  28.2 us
    pallas_call x1, Pallas kernels, local(): pl.pallas_call(finish, out_shape=(jax.ShapeDtypeStruct(flat, F32), jax.Sh...  0.67 us

profile of v4, /device:TPU:0, one launch (start us, length us, event | category | flops | bytes accessed | tf_op | source)
XLA Modules:
  0.0 29.5 jit_solution(12915572628657240340)
XLA Ops:
  0.6 28.2 %shard_map.104 = (f32[128,128]{1,0:T(8,128)S(1)}, f32[25,512]{1,0:T(8,128)S(1)}) custom-call(s32[64]{0:T(128)} %batch_atom_hbm.1, s32[2048]{0:T(1024)} %owner_slot_hbm.1, s32[2]{0:T(128)} %slot_index_hbm.1, f32[128,128]{1,0:T(8,128)} %bitcast.4, f32[128,128]{1,0:T(8,128)} %bitcast.5, f32[128,128]{1,0:T(8,128)} %bitcast.6, f32[25,16384]{1,0:T(8,128)} %basis_hbm.1, ...), custom_call_target="tpu_custom_call" | custom-call | tf_op jit(solution)/shard_map/pallas_call | solution.py:497
  28.9 0.7 %shard_map.105 = (f32[128,128]{1,0:T(8,128)}, f32[25,512]{1,0:T(8,128)}) custom-call(f32[128,128]{1,0:T(8,128)S(1)} %get-tuple-element.6.density, f32[25,512]{1,0:T(8,128)S(1)} %get-tuple-element.7.moments), custom_call_target="tpu_custom_call" | custom-call | tf_op jit(solution)/shard_map/pallas_call | solution.py:547

commit v5 on v4

--- a/solution.py
+++ b/solution.py
@@ -90,7 +90,6 @@
     rho,
     res,
     fresh,
-    fresh_w,
     row_bufs,
     sent_moments,
     all_moments,
@@ -100,7 +99,6 @@
     halves,
     hist_moments,
     base_rows,
-    correct,
     batch_atom,
     owner_slot,
     slot_index,
@@ -132,7 +130,8 @@
 
     plane = min(chips, (members // 2) ** 2)
     chip_steps = [z * plane + p for p in reversed(range(plane)) for z in reversed(range(chips // plane))]
-    device_steps = [2 * step + c for step in chip_steps for c in (1, 0)][:-1]
+    device_steps = [2 * step + c for c in (0, 1) for step in chip_steps]
+    device_steps.remove(0)
 
     barrier = pltpu.get_barrier_semaphore()
 
@@ -284,10 +283,8 @@
             slot = slot_index[iteration - 1]
             replaced = sub == slot
 
-            acc = [jnp.zeros((SUBS, LANES), F32) for _ in range(4)]
-            for t in range(tiles):
-                acc[t % 4] = acc[t % 4] + fresh_w[t : t + 1, :] * res[:, t * LANES : (t + 1) * LANES]
             acc = (acc[0] + acc[1]) + (acc[2] + acc[3])
+            square = jnp.sum(square, axis=0, keepdims=True)
             acc = jnp.where(replaced, square, acc)
             packed = jnp.where(lane == sub, jnp.sum(acc, axis=1, keepdims=True), 0.0)
             row_buf[pl.ds(me, 1)] = jnp.sum(packed, axis=0, keepdims=True)[None]
@@ -441,6 +438,8 @@
         damped = jnp.where(comp < harmonics, at_batch * (mixing_beta / (1.0 + degree)), 0.0)
         spread = jnp.concatenate([jnp.where(spot == turn + 4 * side, damped, 0.0) for side in range(2)], axis=1)
         high, low = split(spread)
+        acc = [jnp.zeros((SUBS, LANES), F32) for _ in range(4)]
+        square = jnp.zeros((SUBS, LANES), F32)
         for g in range(batches // SUBS):
             mine = slice(g * SUBS, (g + 1) * SUBS)
             x = jnp.concatenate([high[mine], low[mine]], axis=0).astype(jnp.bfloat16)
@@ -451,21 +450,22 @@
                 out = part if out is None else out + part
             out = out[0:SUBS] + out[SUBS:]
             for v in range(per_batch):
-                correct[pl.ds(g * SUBS * per_batch + v, SUBS, stride=per_batch), :] = out[
-                    :, v * LANES : (v + 1) * LANES
-                ]
-        density = base_rows[...] - correct[...]
-        density_out[...] = density
+                lines = pl.ds(g * SUBS * per_batch + v, SUBS, stride=per_batch)
+                density = base_rows[lines, :] - out[:, v * LANES : (v + 1) * LANES]
+                density_out[lines, :] = density
+                if not last:
+                    new = target[lines, :] + coupling[lines, :] * jnp.tanh(density) - density
+                    new_w = new * w[lines, :]
+                    fresh[lines, :] = new
+                    square = square + new * new_w
+                    for k in range(SUBS):
+                        t = (g * SUBS + k) * per_batch + v
+                        line = jnp.broadcast_to(new_w[k : k + 1, :], (SUBS, LANES))
+                        acc[k % 4] = acc[k % 4] + line * res[:, t * LANES : (t + 1) * LANES]
         if last:
             turned = jnp.transpose(own_sum[...])
             final = (turned[0:32] + turned[32:64]) + (turned[64:96] + turned[96:128])
             moments_out[...] = final[0:harmonics] * scale
-        if not last:
-            new = target[...] + coupling[...] * jnp.tanh(density) - density
-            new_w = new * w[...]
-            fresh[...] = new
-            fresh_w[...] = new_w
-            square = jnp.sum(new * new_w, axis=0, keepdims=True)
 
 
 def finish(density, moments, density_out, moments_out, sem):
@@ -507,7 +507,6 @@
             pltpu.VMEM((hist_len, points), F32),
             pltpu.VMEM((hist_len, points), F32),
             pltpu.VMEM(flat, F32),
-            pltpu.VMEM(flat, F32),
             pltpu.VMEM((iters, devices, 1, LANES), F32),
             pltpu.VMEM((iters, batches // 4, LANES), F32),
             pltpu.VMEM((iters, 2, devices // 2, batches // 4, LANES), F32),
@@ -516,7 +515,6 @@
             pltpu.VMEM((owned, LANES), F32),
             pltpu.VMEM((2, batches * 32, points // batches), jnp.bfloat16),
             pltpu.VMEM((batches // 4, SUBS, LANES), F32),
-            pltpu.VMEM(flat, F32),
             pltpu.VMEM(flat, F32),
             pltpu.SMEM(batch_atom.shape, batch_atom.dtype),
             pltpu.SMEM(owner_slot.shape, owner_slot.dtype),

time: 29.7 us -> 29.7 us (level)
  no operation moved by 1% of the time
where the time goes in v5:
time: 29.7 us; the launch traced here: 29.5 us
  Pallas kernels  28.9 us (97%)
  between operations  0.64 us (2%)
    pallas_call x1, Pallas kernels, local(): pl.pallas_call(functools.partial(kernel, cfg), out_shape=(jax.ShapeDtypeS...  28.2 us
    pallas_call x1, Pallas kernels, local(): pl.pallas_call(finish, out_shape=(jax.ShapeDtypeStruct(flat, F32), jax.Sh...  0.67 us

profile of v5, /device:TPU:0, one launch (start us, length us, event | category | flops | bytes accessed | tf_op | source)
XLA Modules:
  0.0 29.5 jit_solution(2434862303174714050)
XLA Ops:
  0.6 28.2 %shard_map.104 = (f32[128,128]{1,0:T(8,128)S(1)}, f32[25,512]{1,0:T(8,128)S(1)}) custom-call(s32[64]{0:T(128)} %batch_atom_hbm.1, s32[2048]{0:T(1024)} %owner_slot_hbm.1, s32[2]{0:T(128)} %slot_index_hbm.1, f32[128,128]{1,0:T(8,128)} %bitcast.4, f32[128,128]{1,0:T(8,128)} %bitcast.5, f32[128,128]{1,0:T(8,128)} %bitcast.6, f32[25,16384]{1,0:T(8,128)} %basis_hbm.1, ...), custom_call_target="tpu_custom_call" | custom-call | tf_op jit(solution)/shard_map/pallas_call | solution.py:497
  28.8 0.7 %shard_map.105 = (f32[128,128]{1,0:T(8,128)}, f32[25,512]{1,0:T(8,128)}) custom-call(f32[128,128]{1,0:T(8,128)S(1)} %get-tuple-element.6.density, f32[25,512]{1,0:T(8,128)S(1)} %get-tuple-element.7.moments), custom_call_target="tpu_custom_call" | custom-call | tf_op jit(solution)/shard_map/pallas_call | solution.py:545

commit v6 on v5

--- a/solution.py
+++ b/solution.py
@@ -288,7 +288,7 @@
             acc = jnp.where(replaced, square, acc)
             packed = jnp.where(lane == sub, jnp.sum(acc, axis=1, keepdims=True), 0.0)
             row_buf[pl.ds(me, 1)] = jnp.sum(packed, axis=0, keepdims=True)[None]
-        wait = exchange_rows(row_buf, row_sem.at[iteration])
+        wait = exchange_rows(row_buf, row_sem)
 
         if iteration == 0:
             loads[2].wait()
@@ -357,7 +357,7 @@
 
         mixed = [jnp.sum(coeff_col * hist_moments[r], axis=0, keepdims=True) for r in range(rows)]
         sent_buf[...] = jnp.concatenate(mixed, axis=0)
-        wait_landed, wait_passed = exchange_moments(sent_buf, moment_buf, moment_sem.at[iteration], last)
+        wait_landed, wait_passed = exchange_moments(sent_buf, moment_buf, moment_sem, last)
 
         if iteration == 0:
             base = (my_member * owned).astype(F32)
@@ -395,12 +395,14 @@
             return jnp.concatenate([piece.astype(jnp.bfloat16) for piece in split(everywhere)], axis=1)
 
         def near_part(pieces, side):
-            out = jnp.dot(near[:, side * depth : (side + 1) * depth], pieces, preferred_element_type=F32)
-            out = out[:, 0:LANES] + out[:, LANES:]
             group = lax.broadcasted_iota(jnp.int32, (batches, LANES), 1) // 32
-            total = out[0:batches]
-            for q in range(1, 4):
-                total = jnp.where(group == q, out[q * batches : (q + 1) * batches], total)
+            total = None
+            for half in range(2):
+                lines = slice(2 * half * batches, 2 * (half + 1) * batches)
+                out = jnp.dot(near[lines, side * depth : (side + 1) * depth], pieces, preferred_element_type=F32)
+                out = out[:, 0:LANES] + out[:, LANES:]
+                pair = jnp.where(group % 2 == 0, out[0:batches], out[batches:])
+                total = pair if half == 0 else jnp.where(group // 2 == 0, total, pair)
             return total
 
         def own_part(pieces, side):
@@ -520,8 +522,8 @@
             pltpu.SMEM(owner_slot.shape, owner_slot.dtype),
             pltpu.SMEM(slot_index.shape, slot_index.dtype),
             pltpu.SemaphoreType.DMA((9,)),
-            pltpu.SemaphoreType.DMA((iters, 2)),
-            pltpu.SemaphoreType.DMA((iters, 4, 2)),
+            pltpu.SemaphoreType.DMA((2,)),
+            pltpu.SemaphoreType.DMA((4, 2)),
         ],
         compiler_params=pltpu.CompilerParams(
             collective_id=0, has_side_effects=True, vmem_limit_bytes=40 * 1024 * 1024

time: 29.7 us -> 29.5 us (level)
  no operation moved by 1% of the time
where the time goes in v6:
time: 29.5 us; the launch traced here: 29.4 us
  Pallas kernels  28.7 us (97%)
  between operations  0.64 us (2%)
    pallas_call x1, Pallas kernels, local(): pl.pallas_call(functools.partial(kernel, cfg), out_shape=(jax.ShapeDtypeS...  28 us
    pallas_call x1, Pallas kernels, local(): pl.pallas_call(finish, out_shape=(jax.ShapeDtypeStruct(flat, F32), jax.Sh...  0.67 us

profile of v6, /device:TPU:0, one launch (start us, length us, event | category | flops | bytes accessed | tf_op | source)
XLA Modules:
  0.0 29.4 jit_solution(5184521368691557645)
XLA Ops:
  0.6 28.0 %shard_map.104 = (f32[128,128]{1,0:T(8,128)S(1)}, f32[25,512]{1,0:T(8,128)S(1)}) custom-call(s32[64]{0:T(128)} %batch_atom_hbm.1, s32[2048]{0:T(1024)} %owner_slot_hbm.1, s32[2]{0:T(128)} %slot_index_hbm.1, f32[128,128]{1,0:T(8,128)} %bitcast.4, f32[128,128]{1,0:T(8,128)} %bitcast.5, f32[128,128]{1,0:T(8,128)} %bitcast.6, f32[25,16384]{1,0:T(8,128)} %basis_hbm.1, ...), custom_call_target="tpu_custom_call" | custom-call | tf_op jit(solution)/shard_map/pallas_call | solution.py:499
  28.7 0.7 %shard_map.105 = (f32[128,128]{1,0:T(8,128)}, f32[25,512]{1,0:T(8,128)}) custom-call(f32[128,128]{1,0:T(8,128)S(1)} %get-tuple-element.6.density, f32[25,512]{1,0:T(8,128)S(1)} %get-tuple-element.7.moments), custom_call_target="tpu_custom_call" | custom-call | tf_op jit(solution)/shard_map/pallas_call | solution.py:547

commit v7 on v6

--- a/solution.py
+++ b/solution.py
@@ -357,7 +357,7 @@
 
         mixed = [jnp.sum(coeff_col * hist_moments[r], axis=0, keepdims=True) for r in range(rows)]
         sent_buf[...] = jnp.concatenate(mixed, axis=0)
-        wait_landed, wait_passed = exchange_moments(sent_buf, moment_buf, moment_sem, last)
+        wait_landed, wait_passed = exchange_moments(sent_buf, moment_buf, moment_sem, True)
 
         if iteration == 0:
             base = (my_member * owned).astype(F32)

time: 29.5 us -> 29.5 us (level)
  no operation moved by 1% of the time
where the time goes in v7:
time: 29.5 us; the launch traced here: 29.4 us
  Pallas kernels  28.7 us (97%)
  between operations  0.64 us (2%)
    pallas_call x1, Pallas kernels, local(): pl.pallas_call(functools.partial(kernel, cfg), out_shape=(jax.ShapeDtypeS...  28 us
    pallas_call x1, Pallas kernels, local(): pl.pallas_call(finish, out_shape=(jax.ShapeDtypeStruct(flat, F32), jax.Sh...  0.67 us

profile of v7, /device:TPU:0, one launch (start us, length us, event | category | flops | bytes accessed | tf_op | source)
XLA Modules:
  0.0 29.4 jit_solution(11188831340651369059)
XLA Ops:
  0.6 28.0 %shard_map.104 = (f32[128,128]{1,0:T(8,128)S(1)}, f32[25,512]{1,0:T(8,128)S(1)}) custom-call(s32[64]{0:T(128)} %batch_atom_hbm.1, s32[2048]{0:T(1024)} %owner_slot_hbm.1, s32[2]{0:T(128)} %slot_index_hbm.1, f32[128,128]{1,0:T(8,128)} %bitcast.4, f32[128,128]{1,0:T(8,128)} %bitcast.5, f32[128,128]{1,0:T(8,128)} %bitcast.6, f32[25,16384]{1,0:T(8,128)} %basis_hbm.1, ...), custom_call_target="tpu_custom_call" | custom-call | tf_op jit(solution)/shard_map/pallas_call | solution.py:499
  28.7 0.7 %shard_map.105 = (f32[128,128]{1,0:T(8,128)}, f32[25,512]{1,0:T(8,128)}) custom-call(f32[128,128]{1,0:T(8,128)S(1)} %get-tuple-element.6.density, f32[25,512]{1,0:T(8,128)S(1)} %get-tuple-element.7.moments), custom_call_target="tpu_custom_call" | custom-call | tf_op jit(solution)/shard_map/pallas_call | solution.py:547
